TPU v7x, 32 devices: a whole 2x2x4 slice. The times are simulated.
32 devices in a mesh: seq: 8 (over z, core), head: 4 (over y, x).
Axes of the slice: x: 2, y: 2, z: 4, core: 2. Of those that a mesh axis runs over, the one named last changes fastest.
Arguments:
- queries: bfloat16 [4096, 1024], P('seq', 'head'), may hold values from -6 to 6
- keys: bfloat16 [4096, 256], P(('seq', 'head')), may hold values from -6 to 6
- values: bfloat16 [4096, 256], P(('seq', 'head')), may hold values from -3 to 3
- attn_out: bfloat16 [4096, 1024], P('seq', 'head'), may hold values from -1.796875 to 1.796875
- out_grad: bfloat16 [4096, 1024], P('seq', 'head'), may hold values from -6 to 6
- log_norm: float32 [8, 4096], P('head', 'seq'), may hold values from 3.5 to 5.5
- block_layout: int32 [8, 32, 32], P('head'), may hold values 0 or 1
- document_ids: int32 [4096], replicated, may hold values from 0 to 7, never falling along the last dimension, each value on 1 to 2048 neighbouring positions
- block_order: int32 [32], replicated, may hold values from 0 to 31, each once
Outputs:
- query_grad: float32 [4096, 1024], P('seq', 'head')
- key_grad: float32 [4096, 256], P(('seq', 'head'))
- value_grad: float32 [4096, 256], P(('seq', 'head'))
Inputs may be any that keep to these rules, and one draw needn't show every extreme that they name: `document_ids`: never falls along the sequence position; each document covers 1 to 2048 positions, one exactly 2048. `block_order`: each sequence block once.
All inputs are finite; a program needn't handle non-finite values.
Results may differ from a plain program's by a relative error of at most 0.0029.
Values may be sent and summed in bfloat16 or wider, within the bound.
A program may use at most 128 MiB of HBM per device.

v0:
```python
import functools
import math

import jax
import jax.numpy as jnp
from jax import lax
from jax.experimental import pallas as pl
from jax.experimental.pallas import tpu as pltpu
from jax.sharding import PartitionSpec as P

D_HEAD = 128
GROUP = 4
BLOCK = 128
DOCS = 8
CORES = 2
PAIR = 2
REACH = 3
LOG2E = math.log2(math.e)
SCALE = D_HEAD ** -0.5
NT = (((1,), (1,)), ((), ()))
TN = (((0,), (0,)), ((), ()))


def place(share):
    seq, head = lax.axis_index("seq"), lax.axis_index("head")
    return seq // CORES, seq % CORES, head // share, head % share


def remote(src, dst, send, recv, seq, head):
    return pltpu.make_async_remote_copy(
        src_ref=src, dst_ref=dst, send_sem=send, recv_sem=recv,
        device_id={"seq": seq, "head": head}, device_id_type=pl.DeviceIdType.MESH)


def landed(where, sem):
    pltpu.make_async_copy(where, where, sem).wait()


def when(there, run):
    if there is True:
        run()
    else:
        pl.when(there)(run)


def span(index, rows):
    return pl.ds(pl.multiple_of(index * rows, rows), rows)


def near(deep, kv_heads, share):
    z, c, g, x = place(share)
    seq, head = z * CORES + c, g * share + x
    peers = [(z * CORES + (c + d) % CORES, head, True) for d in range(1, CORES)]
    peers += [(seq, g * share + (x + d) % share, True) for d in range(1, share)]
    peers += [(seq, (g + d) % kv_heads * share + x, True) for d in range(1, kv_heads)]
    if deep > 1:
        peers += [(seq + CORES, head, z + 1 < deep), (seq - CORES, head, z > 0)]
    return peers


def signal(sem, peers):
    for seq, head, there in peers:
        when(there, lambda: pl.semaphore_signal(
            sem, inc=1, device_id={"seq": seq, "head": head},
            device_id_type=pl.DeviceIdType.MESH))


def count(peers):
    total = 0
    for _, _, there in peers:
        total = total + (1 if there is True else there.astype(jnp.int32))
    return total


def unit_row(u, unit, rows, kv_heads, share):
    z, c, g, x = place(share)
    per = rows // unit
    piece, sub = u // per, u % per
    depth, group = piece // kv_heads, piece % kv_heads
    owner = (depth * CORES + c) * kv_heads * share + group * share + x
    return owner * rows + sub * unit


def gather_kernel(
    deep, kv_heads, share, q_in, do_in, o_in, ln_in, k_in, v_in, lay_in, docs_in, order_in,
    kv, q_all, do_all, stats, lows, tops, lay_far,
    k_buf, v_buf, o_buf, ln_buf, docs, order, layout,
    local, kv_send, kv_recv, v_recv, x_send, x_recv, core_send, core_recv,
):
    z, c, g, x = place(share)
    seq, head = z * CORES + c, g * share + x
    heads, q_rows = ln_in.shape
    rows = k_in.shape[0]
    own = q_rows // BLOCK
    unit = min(rows, BLOCK)
    mine = z * kv_heads + g

    def cols(index):
        return pl.ds(pl.multiple_of(index * D_HEAD, D_HEAD), D_HEAD)

    here = span(c, q_rows)
    pulls = [
        (k_in, k_buf), (v_in, v_buf),
        (k_in.at[:, cols(g)], kv.at[0, span(mine, rows), :]),
        (v_in.at[:, cols(g)], kv.at[1, span(mine, rows), :]),
        (q_in, q_all.at[x, here, :]), (do_in, do_all.at[x, here, :]),
        (o_in, o_buf), (ln_in, ln_buf), (docs_in, docs), (order_in, order),
        (lay_in, layout.at[x]),
    ]
    pulls = [pltpu.make_async_copy(src, dst, local.at[n]) for n, (src, dst) in enumerate(pulls)]
    for pull in pulls:
        pull.start()
    peers = near(deep, kv_heads, share)
    barrier = pltpu.get_barrier_semaphore()
    signal(barrier, peers)
    for pull in pulls[:6]:
        pull.wait()
    pl.semaphore_wait(barrier, count(peers))

    sent = []

    def send(make, there=True):
        sent.append((there, make))
        when(there, lambda: make().start())

    kv_slots = [0]

    def send_kv(src, dst, arrival, to_seq, to_head, there=True):
        slot = kv_slots[0]
        kv_slots[0] += 1
        send(lambda: remote(src, dst, kv_send.at[slot], arrival, to_seq, to_head), there)

    def whole(index):
        return kv.at[:, span(index, rows), :]

    def onward(index, step, there):
        send_kv(whole(index), whole(index), kv_recv.at[index], seq + step * CORES, head, there)

    for d in range(1, kv_heads):
        other = (g + d) % kv_heads
        for n, (ref, arrival) in enumerate(((k_buf, kv_recv.at[mine]), (v_buf, v_recv.at[d - 1]))):
            send_kv(ref.at[:, cols(other)], kv.at[n, span(mine, rows), :], arrival,
                    seq, other * share + x)

    def chunk_of(lane, core, n):
        return [ref.at[lane, pl.ds(core * q_rows + n * BLOCK, BLOCK), :] for ref in (q_all, do_all)]

    def x_slot(d, n, t):
        return ((d - 1) * own + n) * 2 + t

    far_at = (share - 1) * own * 2

    def send_chunk(n):
        for d in range(1, share):
            for t, part in enumerate(chunk_of(x, c, n)):
                slot = x_slot(d, n, t)
                send(functools.partial(remote, part, part, x_send.at[slot], x_recv.at[slot], seq,
                                       g * share + (x + d) % share))

    onward(mine, 1, z + 1 < deep)
    onward(mine, -1, z > 0)
    for d in range(1, share):
        slot = far_at + (d - 1) * 2
        send(functools.partial(remote, lay_in, lay_far.at[d - 1], x_send.at[slot],
                               x_recv.at[slot], seq, g * share + (x + d) % share))
    send_chunk(0)
    partner = z * CORES + 1 - c
    for n, ref in enumerate((q_all, do_all)):
        part = ref.at[x, here, :]
        send(functools.partial(remote, part, part, core_send.at[n], core_recv.at[n],
                               partner, head))

    for pull in pulls[6:]:
        pull.wait()
    mine_stats = stats.at[x, pl.ds(c * own, own)]
    for n in range(own):
        part = slice(n * BLOCK, (n + 1) * BLOCK)
        at = pl.ds(c * q_rows + n * BLOCK, BLOCK)
        for h in range(heads):
            lanes = slice(h * D_HEAD, (h + 1) * D_HEAD)
            product = (do_all[x, at, lanes].astype(jnp.float32)
                       * o_buf[part, lanes].astype(jnp.float32))
            stats[x, c * own + n, h:h + 1, :] = ln_buf[h:h + 1, part] * LOG2E
            stats[x, c * own + n, heads + h:heads + h + 1, :] = jnp.sum(
                product.T, axis=0, keepdims=True)
    for d in range(1, share):
        slot = far_at + (d - 1) * 2 + 1
        send(functools.partial(remote, mine_stats, mine_stats, x_send.at[slot], x_recv.at[slot],
                               seq, g * share + (x + d) % share))
    send(functools.partial(remote, mine_stats, mine_stats, core_send.at[2], core_recv.at[2],
                           partner, head))
    for n in range(1, own):
        send_chunk(n)

    lane_of = lax.broadcasted_iota(jnp.int32, (1, BLOCK), 1)

    def fill_tops(lane):
        def top_row(i, _):
            qb = order[z * CORES * own + i]

            def top_unit(u, _):
                kb = order[unit_row(u, unit, rows, kv_heads, share) // BLOCK]
                for h in range(heads):
                    on = layout[lane, h, qb, kb] == 1
                    at = pl.ds(pl.multiple_of((lane * heads + h) * BLOCK, BLOCK), BLOCK)
                    tops[i, u, :, at] = jnp.where(on, lane_of + qb * BLOCK, -1)
                return 0

            return lax.fori_loop(0, tops.shape[1], top_unit, 0)

        lax.fori_loop(0, tops.shape[0], top_row, 0)

    ids = docs[...]
    low = jnp.zeros_like(ids)
    for d in range(1, DOCS):
        before = jnp.sum(jnp.where(ids < d, 1.0, 0.0), axis=1, keepdims=True)
        before = jnp.sum(before, axis=0, keepdims=True).astype(jnp.int32)
        low = jnp.where(ids >= d, before, low)
    lows[...] = low

    def relay(part, slot):
        landed(part, x_recv.at[slot])
        send(functools.partial(remote, part, part, core_send.at[3 + slot],
                               core_recv.at[3 + slot], partner, head))

    def relay_chunk(n):
        for d in range(1, share):
            for t, part in enumerate(chunk_of((x - d + share) % share, c, n)):
                relay(part, x_slot(d, n, t))

    for j in range(1, kv_heads):
        index = z * kv_heads + (g + j) % kv_heads
        for n, sem in enumerate((kv_recv.at[index], v_recv.at[kv_heads - j - 1])):
            landed(kv.at[n, span(index, rows), :], sem)
        onward(index, 1, z + 1 < deep)
        onward(index, -1, z > 0)
    chunks = 0
    for d in range(1, deep):
        for j in range(kv_heads):
            for depth, step, here_too in ((z - d, 1, z - d >= 0), (z + d, -1, z + d < deep)):
                index = depth * kv_heads + (g + j) % kv_heads
                when(here_too, functools.partial(
                    lambda index: landed(whole(index), kv_recv.at[index]), index))
                if d < deep - 1:
                    more = z + 1 < deep if step == 1 else z > 0
                    onward(index, step, here_too & more)
        if d == 1:
            fill_tops(x)
        if d == min(2, deep - 1):
            for e in range(1, share):
                lane = (x - e + share) % share
                landed(lay_far.at[e - 1], x_recv.at[far_at + (e - 1) * 2])
                pull = pltpu.make_async_copy(lay_far.at[e - 1], layout.at[lane],
                                             local.at[len(pulls) + e - 1])
                pull.start()
                pull.wait()
                relay(stats.at[lane, pl.ds(c * own, own)], far_at + (e - 1) * 2 + 1)
                fill_tops(lane)
        if chunks < own:
            relay_chunk(chunks)
            chunks += 1
    for n in range(chunks, own):
        relay_chunk(n)
    there = span(1 - c, q_rows)
    for n, ref in enumerate((q_all, do_all)):
        landed(ref.at[x, there, :], core_recv.at[n])
    landed(stats.at[x, pl.ds((1 - c) * own, own)], core_recv.at[2])
    for d in range(1, share):
        lane = (x - d + share) % share
        for n in range(own):
            for t, part in enumerate(chunk_of(lane, 1 - c, n)):
                landed(part, core_recv.at[3 + x_slot(d, n, t)])
        landed(stats.at[lane, pl.ds((1 - c) * own, own)],
               core_recv.at[3 + far_at + (d - 1) * 2 + 1])
    for there, make in sent:
        when(there, functools.partial(lambda make: make().wait_send(), make))


def gather(queries, out_grad, attn_out, log_norm, keys, values, block_layout, document_ids,
           block_order, deep, kv_heads, share):
    rows = keys.shape[0]
    heads, q_rows = log_norm.shape
    blocks = block_order.shape[0]
    own = q_rows // BLOCK
    unit = min(rows, BLOCK)
    pieces = deep * kv_heads
    kv_rows = pieces * rows
    hbm = pl.BlockSpec(memory_space=pltpu.HBM)
    vmem = pl.BlockSpec(memory_space=pltpu.VMEM)
    lanes = share - 1
    x_copies = max(1, lanes * own * 2 + lanes * 2)
    kv_copies = max(1, 2 * (kv_heads - 1) + 2 * kv_heads * (deep - 1))
    dma = pltpu.SemaphoreType.DMA
    every = jax.ShapeDtypeStruct((share, CORES * q_rows, heads * D_HEAD), queries.dtype)
    return pl.pallas_call(
        functools.partial(gather_kernel, deep, kv_heads, share),
        out_shape=(
            jax.ShapeDtypeStruct((2, kv_rows, D_HEAD), keys.dtype),
            every,
            every,
            jax.ShapeDtypeStruct((share, CORES * own, 2 * heads, BLOCK), jnp.float32),
            jax.ShapeDtypeStruct((blocks, BLOCK), jnp.int32),
            jax.ShapeDtypeStruct(
                (CORES * own, kv_rows // unit, 1, share * heads * BLOCK), jnp.int32),
            jax.ShapeDtypeStruct((max(1, lanes),) + block_layout.shape, jnp.int32),
        ),
        in_specs=[hbm] * 9,
        out_specs=(vmem,) * 6 + (hbm,),
        scratch_shapes=[
            pltpu.VMEM(keys.shape, keys.dtype),
            pltpu.VMEM(values.shape, values.dtype),
            pltpu.VMEM(attn_out.shape, attn_out.dtype),
            pltpu.VMEM(log_norm.shape, jnp.float32),
            pltpu.VMEM((blocks, BLOCK), jnp.int32),
            pltpu.SMEM((blocks,), jnp.int32),
            pltpu.SMEM((share,) + block_layout.shape, jnp.int32),
            dma((11 + max(1, lanes),)),
            dma((kv_copies,)),
            dma((pieces,)),
            dma((max(1, kv_heads - 1),)),
            dma((x_copies,)),
            dma((x_copies,)),
            dma((3 + x_copies,)),
            dma((3 + x_copies,)),
        ],
        compiler_params=pltpu.CompilerParams(collective_id=0, has_side_effects=True,
            vmem_limit_bytes=16 << 20),
        name="gather",
    )(*[pltpu.with_memory_space_constraint(array, pltpu.HBM) for array in (
        queries, out_grad, attn_out, log_norm, keys, values, block_layout,
        document_ids.reshape(blocks, BLOCK), block_order)])


def grads_kernel(
    kv_heads, share, rows, order_in, docs_in, q_all, do_all, stats, kv, lows, tops,
    dqt, acc, order, docs, unit_pos, item_q, item_u, low_bits, local,
):
    z, c, g, x = place(share)
    queries = dqt.shape[1]
    heads = q_all.shape[2] // D_HEAD
    unit = min(rows, BLOCK)
    units = kv.shape[1] // unit
    first = z * queries
    pulls = [pltpu.make_async_copy(order_in, order, local.at[0]),
             pltpu.make_async_copy(docs_in, docs, local.at[1])]
    for pull in pulls:
        pull.start()
    acc[...] = jnp.zeros_like(acc)

    def clear(i, _):
        for s in range(share):
            dqt[s, pl.ds(i, 1)] = jnp.zeros((1,) + dqt.shape[2:], jnp.float32)
        return 0

    lax.fori_loop(0, queries, clear, 0)
    for pull in pulls:
        pull.wait()

    for u in range(units):
        row = unit_row(u, unit, rows, kv_heads, share)
        unit_pos[u] = order[row // BLOCK] * BLOCK + row % BLOCK

    def listing(i, n):
        qb = order[first + i]
        doc = docs[qb * BLOCK]
        for u in range(units):
            pos = unit_pos[u]
            seen = (pos <= qb * BLOCK + BLOCK - 1) & (docs[pos + unit - 1] >= doc)
            item_q[n] = i
            item_u[n] = u
            n = n + seen.astype(jnp.int32)
        return n

    total = lax.fori_loop(0, queries, listing, 0)
    wide = share * heads * BLOCK
    sub = lax.broadcasted_iota(jnp.int32, (unit, wide), 0)
    low_bits[...] = jnp.zeros_like(low_bits)
    for n in range(2 * PAIR):
        item_q[total + n] = 0
        item_u[total + n] = 0

    def stacked(ref, i):
        at = pl.ds(pl.multiple_of(i * BLOCK, BLOCK), BLOCK)
        return jnp.concatenate(
            [ref[s, at, h * D_HEAD:(h + 1) * D_HEAD] for s in range(share) for h in range(heads)],
            axis=0)

    def weigh(n, slot):
        i, u = item_q[n], item_u[n]
        pos = unit_pos[u]
        at = pl.ds(pl.multiple_of(u * unit, unit), unit)
        k, v = kv[0, at, :], kv[1, at, :]
        q4, do4 = stacked(q_all, i), stacked(do_all, i)
        rowed = [stats[s, i] for s in range(share)]
        norm = jnp.concatenate([r[h:h + 1] for r in rowed for h in range(heads)], axis=1)
        delta = jnp.concatenate(
            [r[heads + h:heads + h + 1] for r in rowed for h in range(heads)], axis=1)
        low = jnp.concatenate([lows[pl.ds(order[first + i], 1), :]] * (share * heads), axis=1)
        top = jnp.where(n < total, tops[i, u], -1)
        keep = (sub >= low - pos) & (sub <= top - pos)
        st = lax.dot_general(k, q4, NT, preferred_element_type=jnp.float32)
        dpt = lax.dot_general(v, do4, NT, preferred_element_type=jnp.float32)
        w = jnp.where(keep, jnp.exp2(st * (SCALE * LOG2E) - norm), 0.0)
        low_bits[slot, 0] = w.astype(jnp.bfloat16)
        low_bits[slot, 1] = (w * (dpt - delta)).astype(jnp.bfloat16)

    def collect(n, slot):
        i, u = item_q[n], item_u[n]
        at = pl.ds(pl.multiple_of(u * unit, unit), unit)
        q4, do4 = stacked(q_all, i), stacked(do_all, i)
        ds = low_bits[slot, 1]
        dv = jnp.dot(low_bits[slot, 0], do4, preferred_element_type=jnp.float32)
        dk = jnp.dot(ds, q4, preferred_element_type=jnp.float32)
        dq = lax.dot_general(kv[0, at, :], ds, TN, preferred_element_type=jnp.float32)
        return i, at, dk, dv, dq

    def step(t, _):
        before = jnp.maximum(t - 1, 0) * PAIR
        done = [collect(before + n, n) for n in range(PAIR)]
        for n in range(PAIR):
            weigh(t * PAIR + n, n)
        for i, at, dk, dv, dq in done:
            acc[0, at, :] += dk
            acc[1, at, :] += dv
            for s in range(share):
                dqt[s, i] += dq[:, s * heads * BLOCK:(s + 1) * heads * BLOCK]
        return 0

    lax.fori_loop(0, (total + PAIR - 1) // PAIR + 1, step, 0)


def local_grads(block_order, document_ids, q_all, do_all, stats, kv, lows, tops, rows, kv_heads,
                share):
    heads = q_all.shape[2] // D_HEAD
    queries, units = tops.shape[:2]
    hbm = pl.BlockSpec(memory_space=pltpu.HBM)
    vmem = pl.BlockSpec(memory_space=pltpu.VMEM)
    return pl.pallas_call(
        functools.partial(grads_kernel, kv_heads, share, rows),
        out_shape=(
            jax.ShapeDtypeStruct((share, queries, D_HEAD, heads * BLOCK), jnp.float32),
            jax.ShapeDtypeStruct(kv.shape, jnp.float32),
        ),
        in_specs=[hbm] * 2 + [vmem] * 6,
        out_specs=(vmem, vmem),
        scratch_shapes=[
            pltpu.SMEM(block_order.shape, jnp.int32),
            pltpu.SMEM(document_ids.shape, jnp.int32),
            pltpu.SMEM((units,), jnp.int32),
            pltpu.SMEM((queries * units + 2 * PAIR,), jnp.int32),
            pltpu.SMEM((queries * units + 2 * PAIR,), jnp.int32),
            pltpu.VMEM((PAIR, 2, min(rows, BLOCK), share * heads * BLOCK), jnp.bfloat16),
            pltpu.SemaphoreType.DMA((2,)),
        ],
        compiler_params=pltpu.CompilerParams(vmem_limit_bytes=24 << 20),
        name="grads",
    )(pltpu.with_memory_space_constraint(block_order, pltpu.HBM),
      pltpu.with_memory_space_constraint(document_ids, pltpu.HBM),
      q_all, do_all, stats, kv, lows, tops)


def scatter_kernel(
    deep, kv_heads, share, rows, acc, dqt, kv_in, dq_sum, dq_in,
    kv_out, joined, dq_core, dq_out, ready, kv_send, kv_recv, join_recv, core_send, core_recv,
    x_send, x_recv,
):
    z, c, g, x = place(share)
    seq, head = z * CORES + c, g * share + x
    partner = z * CORES + 1 - c
    own = dqt.shape[1] // CORES
    heads = dqt.shape[3] // BLOCK
    mine = z * kv_heads + g
    peers = near(deep, kv_heads, share)
    barrier = pltpu.get_barrier_semaphore()
    signal(barrier, peers)
    for p in range(deep * kv_heads):
        part = slice(p * rows, (p + 1) * rows)
        kv_out[p, 0] = (acc[0, part, :] * SCALE).astype(jnp.bfloat16)
        kv_out[p, 1] = acc[1, part, :].astype(jnp.bfloat16)
    kv_in[mine] = kv_out[mine]
    for depth in range(deep):
        def unused(depth=depth):
            at = pl.ds(depth * kv_heads, kv_heads)
            kv_in[at] = jnp.zeros((kv_heads,) + kv_in.shape[1:], kv_in.dtype)

        if depth >= REACH or depth < deep - REACH:
            pl.when((depth - z >= REACH) | (z - depth >= REACH))(unused)
    pl.semaphore_wait(barrier, count(peers))

    sent = []

    def send(make, there=True):
        sent.append((there, make))
        when(there, lambda: make().start())

    slots = [0]

    def slot_of():
        slots[0] += 1
        return slots[0] - 1

    def inside(depth):
        return (depth >= 0) & (depth < deep)

    def give(step, turn, there=True):
        slot = slot_of()
        depth, group = z + step, (g + turn) % kv_heads
        index = depth * kv_heads + group
        send(functools.partial(remote, kv_out.at[index], kv_in.at[mine], kv_send.at[slot],
                               kv_recv.at[mine], depth * CORES + c, group * share + x), there)

    def join(index):
        landed(joined.at[index], join_recv.at[index])
        at = span(index, rows)
        for n, factor in enumerate((SCALE, 1.0)):
            kv_out[index, n] = (acc[n, at, :] * factor
                                + joined[index, n].astype(jnp.float32)).astype(jnp.bfloat16)

    def blocks_of(core, n):
        return dqt.at[:, pl.ds(core * own + n, 1)]

    for far in range(deep - 1, REACH - 1, -1):
        for depth, step in ((far, 1), (deep - 1 - far, -1)):
            away = (depth - z) * step >= REACH
            behind = (z > 0) if step == 1 else (z + 1 < deep)
            for turn in range(kv_heads):
                index = depth * kv_heads + (g + turn) % kv_heads
                if far > REACH:
                    pl.when(away & behind)(functools.partial(join, index))
                slot = slot_of()
                send(functools.partial(remote, kv_out.at[index], joined.at[index],
                                       kv_send.at[slot], join_recv.at[index],
                                       (z + step) * CORES + c, head), away)
    if deep > 1:
        give(1, 0, z + 1 < deep)
        give(-1, 0, z > 0)
    for turn in range(1, kv_heads):
        give(0, turn)
    for n in range(own):
        send(functools.partial(remote, blocks_of(1 - c, n), dq_core.at[:, pl.ds(n, 1)],
                               core_send.at[n], core_recv.at[n], partner, head))
    along = peers[-2:] if deep > 1 else []
    near_end = {1: z == 0, -1: z == deep - 1}
    for d in range(1, min(REACH, deep)):
        signal(ready.at[d - 1], along)
        pl.semaphore_wait(ready.at[d - 1], count(along))
        for step in (1, -1):
            for turn in range(1, kv_heads):
                there = inside(z + step * d)
                give(step * d, turn, there & near_end[step] if d == REACH - 1 else there)
            if d + 1 < min(REACH, deep):
                there = inside(z + step * (d + 1))
                give(step * (d + 1), 0, there & near_end[step] if d == REACH - 2 else there)

    def query_block(n):
        landed(dq_core.at[:, pl.ds(n, 1)], core_recv.at[n])
        at = slice(n * BLOCK, (n + 1) * BLOCK)
        for d in range(share - 1, -1, -1):
            lane = (x + d) % share
            total = (dqt[lane, c * own + n] + dq_core[lane, n]) * SCALE
            for h in range(heads):
                flat = total[:, h * BLOCK:(h + 1) * BLOCK].T
                if d:
                    dq_out[d - 1, at, h * D_HEAD:(h + 1) * D_HEAD] = flat.astype(jnp.bfloat16)
                else:
                    dq_sum[at, h * D_HEAD:(h + 1) * D_HEAD] = flat
            if d:
                slot = (d - 1) * own + n
                send(functools.partial(
                    remote, dq_out.at[d - 1, at, :], dq_in.at[d - 1, at, :], x_send.at[slot],
                    x_recv.at[slot], seq, g * share + lane))

    early = min(2, own)
    for n in range(early):
        query_block(n)
    if deep >= REACH:
        for turn in range(kv_heads):
            for step in (1, -1):
                depth = z + step * (REACH - 1)
                there = inside(depth) & ~near_end[step]
                index = depth * kv_heads + (g + turn) % kv_heads
                pl.when(there)(functools.partial(join, index))
                give(step * (REACH - 1), turn, there)
    for n in range(early, own):
        query_block(n)
    for depth in range(deep):
        for turn in range(kv_heads):
            index = depth * kv_heads + (g + turn) % kv_heads
            close = (depth - z < REACH) & (z - depth < REACH)
            get = functools.partial(
                lambda index: landed(kv_in.at[index], kv_recv.at[index]), index)
            when(close if turn else close & (depth != z), get)
    for d in range(1, share):
        for n in range(own):
            at = slice(n * BLOCK, (n + 1) * BLOCK)
            landed(dq_in.at[d - 1, at, :], x_recv.at[(d - 1) * own + n])
    for there, make in sent:
        when(there, functools.partial(lambda make: make().wait_send(), make))


def finish_kernel(deep, kv_heads, share, kv_in, dq_sum, dq_in, dq, dk, dv):
    total = dq_sum[...]
    for d in range(share - 1):
        total += dq_in[d].astype(jnp.float32)
    dq[...] = total
    for j in range(kv_heads):
        for n, ref in enumerate((dk, dv)):
            total = kv_in[j, n].astype(jnp.float32)
            for depth in range(1, deep):
                total += kv_in[depth * kv_heads + j, n].astype(jnp.float32)
            ref[:, j * D_HEAD:(j + 1) * D_HEAD] = total


def scatter(dqt, acc, rows, deep, kv_heads, share):
    pieces = deep * kv_heads
    queries, heads = dqt.shape[1], dqt.shape[3] // BLOCK
    own = queries // CORES
    q_rows = own * BLOCK
    vmem = pl.BlockSpec(memory_space=pltpu.VMEM)
    dma = pltpu.SemaphoreType.DMA
    lanes = max(1, share - 1)
    kv_in, dq_sum, dq_in = pl.pallas_call(
        functools.partial(scatter_kernel, deep, kv_heads, share, rows),
        out_shape=(
            jax.ShapeDtypeStruct((pieces, 2, rows, D_HEAD), jnp.bfloat16),
            jax.ShapeDtypeStruct((q_rows, heads * D_HEAD), jnp.float32),
            jax.ShapeDtypeStruct((lanes, q_rows, heads * D_HEAD), jnp.bfloat16),
        ),
        in_specs=[vmem] * 2,
        out_specs=(vmem,) * 3,
        scratch_shapes=[
            pltpu.VMEM((pieces, 2, rows, D_HEAD), jnp.bfloat16),
            pltpu.VMEM((pieces, 2, rows, D_HEAD), jnp.bfloat16),
            pltpu.VMEM((dqt.shape[0], own) + dqt.shape[2:], jnp.float32),
            pltpu.VMEM((lanes, q_rows, heads * D_HEAD), jnp.bfloat16),
            pltpu.SemaphoreType.REGULAR((max(1, deep - 1),)),
            dma((6 * pieces,)),
            dma((pieces,)),
            dma((pieces,)),
            dma((own,)),
            dma((own,)),
            dma((lanes * own,)),
            dma((lanes * own,)),
        ],
        compiler_params=pltpu.CompilerParams(collective_id=1, has_side_effects=True,
            vmem_limit_bytes=20 << 20),
        name="scatter",
    )(acc, dqt)
    grad = jax.ShapeDtypeStruct((rows, kv_heads * D_HEAD), jnp.float32)
    return pl.pallas_call(
        functools.partial(finish_kernel, deep, kv_heads, share),
        out_shape=(jax.ShapeDtypeStruct(dq_sum.shape, jnp.float32), grad, grad),
        in_specs=[vmem] * 3,
        out_specs=(vmem,) * 3,
        compiler_params=pltpu.CompilerParams(vmem_limit_bytes=8 << 20),
        name="finish",
    )(kv_in, dq_sum, dq_in)


def body(
    queries, keys, values, attn_out, out_grad, log_norm, block_layout, document_ids, block_order
):
    share = GROUP // log_norm.shape[0]
    kv_heads = lax.axis_size("head") // share
    deep = lax.axis_size("seq") // CORES
    rows = keys.shape[0]
    kv, q_all, do_all, stats, lows, tops, _ = gather(
        queries, out_grad, attn_out, log_norm, keys, values, block_layout, document_ids,
        block_order, deep, kv_heads, share)
    dqt, acc = local_grads(block_order, document_ids, q_all, do_all, stats, kv, lows, tops, rows,
                           kv_heads, share)
    return tuple(scatter(dqt, acc, rows, deep, kv_heads, share))


def solution(mesh):
    in_specs = (
        P("seq", "head"),
        P(("seq", "head"), None),
        P(("seq", "head"), None),
        P("seq", "head"),
        P("seq", "head"),
        P("head", "seq"),
        P("head", None, None),
        P(),
        P(),
    )
    out_specs = (P("seq", "head"), P(("seq", "head"), None), P(("seq", "head"), None))
    return jax.shard_map(body, mesh=mesh, in_specs=in_specs, out_specs=out_specs, check_vma=False)
```

profile of v0, /device:TPU:0, one launch (start us, length us, event | category | flops | bytes accessed | tf_op | source)
XLA Modules:
  0.0 43.5 jit_solution(1909542249363442479)
XLA Ops:
  0.6 20.6 %gather.1 = (bf16[2,1024,128]{2,1,0:T(8,128)(2,1)S(1)}, bf16[2,1024,256]{2,1,0:T(8,128)(2,1)S(1)}, bf16[2,1024,256]{2,1,0:T(8,128)(2,1)S(1)}, f32[2,8,4,128]{3,2...) custom-call(bf16[512,256]{1,0:T(8,128)(2,1)} %q_in.1, ...), custom_call_target="tpu_custom_call" | custom-call | tf_op jit(solution)/shard_map/gather/pallas_call | solution.py:295
  21.3 5.7 %grads.1 = (f32[2,8,128,256]{3,2,1,0:T(8,128)S(1)}, f32[2,1024,128]{2,1,0:T(8,128)S(1)}) custom-call(s32[32]{0:T(128)} %order_in.3, s32[4096]{0:T(1024)} %docs_in.1, bf16[2,1024,256]{2,1,0:T(8,128)(2,1)S(1)} %get-tuple-element.14.q_all, bf16[2,1024,256]{2,1,0:T(8,128)(2,1)S(1)} %get-tuple-element.15.do_all, f32[2,8,4,128]{3,2,1,0:T(4,128)S(1)} %get-tuple-element.16.stats, ...), custom_call_target="tpu_custom_call" | custom-call | tf_op jit(solution)/shard_map/grads/pallas_call | solution.py:438
  26.9 15.6 %scatter.1 = (bf16[8,2,128,128]{3,2,1,0:T(8,128)(2,1)S(1)}, f32[512,256]{1,0:T(8,128)S(1)}, bf16[1,512,256]{2,1,0:T(8,128)(2,1)S(1)}) custom-call(f32[2,1024,128]{2,1,0:T(8,128)S(1)} %get-tuple-element.20.acc, f32[2,8,128,256]{3,2,1,0:T(8,128)S(1)} %get-tuple-element.21.dqt), custom_call_target="tpu_custom_call" | custom-call | tf_op jit(solution)/shard_map/scatter/pallas_call | solution.py:622
  42.6 0.9 %finish.1 = (f32[512,256]{1,0:T(8,128)}, f32[128,256]{1,0:T(8,128)}, f32[128,256]{1,0:T(8,128)}) custom-call(bf16[8,2,128,128]{3,2,1,0:T(8,128)(2,1)S(1)} %get-tuple-element.22.kv_in, f32[512,256]{1,0:T(8,128)S(1)} %get-tuple-element.23.dq_sum, bf16[1,512,256]{2,1,0:T(8,128)(2,1)S(1)} %get-tuple-element.24.dq_in), custom_call_target="tpu_custom_call" | custom-call | tf_op jit(solution)/shard_map/finish/pallas_call | solution.py:650
where the time goes:
time: 43.3 us; the launch traced here: 43.5 us
  Pallas kernels  42.8 us (99%)
  between operations  0.66 us (2%)
    pallas_call x1, Pallas kernels, gather(): pl.pallas_call(functools.partial(gather_kernel, deep, kv_heads, share), o...  20.6 us
    pallas_call x1, Pallas kernels, scatter(): pl.pallas_call(functools.partial(scatter_kernel, deep, kv_heads, share, r...  15.6 us
    pallas_call x1, Pallas kernels, local_grads(): pl.pallas_call(functools.partial(grads_kernel, kv_heads, share, rows), ou...  5.65 us
    pallas_call x1, Pallas kernels, scatter(): pl.pallas_call(functools.partial(finish_kernel, deep, kv_heads, share), o...  0.93 us

commit v1 on v0

--- a/solution.py
+++ b/solution.py
@@ -13,7 +13,8 @@
 BLOCK = 128
 DOCS = 8
 CORES = 2
-PAIR = 2
+PAIR = 4
+SPAN = 2
 REACH = 3
 LOG2E = math.log2(math.e)
 SCALE = D_HEAD ** -0.5
@@ -83,9 +84,9 @@
 
 def gather_kernel(
     deep, kv_heads, share, q_in, do_in, o_in, ln_in, k_in, v_in, lay_in, docs_in, order_in,
-    kv, q_all, do_all, stats, lows, tops, lay_far,
-    k_buf, v_buf, o_buf, ln_buf, docs, order, layout,
-    local, kv_send, kv_recv, v_recv, x_send, x_recv, core_send, core_recv,
+    kv, q_all, do_all, stats, lows, tops, acc, dq_own,
+    stage, o_buf, ln_buf, docs, order, layout, seen, own_tops, low_bits,
+    local, ready, kv_send, kv_recv, x_send, x_recv, core_send, core_recv,
 ):
     z, c, g, x = place(share)
     seq, head = z * CORES + c, g * share + x
@@ -99,21 +100,21 @@
         return pl.ds(pl.multiple_of(index * D_HEAD, D_HEAD), D_HEAD)
 
     here = span(c, q_rows)
-    pulls = [
-        (k_in, k_buf), (v_in, v_buf),
-        (k_in.at[:, cols(g)], kv.at[0, span(mine, rows), :]),
-        (v_in.at[:, cols(g)], kv.at[1, span(mine, rows), :]),
-        (q_in, q_all.at[x, here, :]), (do_in, do_all.at[x, here, :]),
-        (o_in, o_buf), (ln_in, ln_buf), (docs_in, docs), (order_in, order),
-        (lay_in, layout.at[x]),
-    ]
+    pulls = [(k_in.at[:, cols(g)], kv.at[0, span(mine, rows), :]),
+             (v_in.at[:, cols(g)], kv.at[1, span(mine, rows), :])]
+    for d in range(1, kv_heads):
+        other = cols((g + d) % kv_heads)
+        pulls += [(k_in.at[:, other], stage.at[d - 1, 0]), (v_in.at[:, other], stage.at[d - 1, 1])]
+    pulls += [(q_in, q_all.at[x, here, :]), (do_in, do_all.at[x, here, :])]
+    urgent = len(pulls)
+    pulls += [(order_in, order), (lay_in, layout), (o_in, o_buf), (ln_in, ln_buf), (docs_in, docs)]
     pulls = [pltpu.make_async_copy(src, dst, local.at[n]) for n, (src, dst) in enumerate(pulls)]
     for pull in pulls:
         pull.start()
     peers = near(deep, kv_heads, share)
     barrier = pltpu.get_barrier_semaphore()
     signal(barrier, peers)
-    for pull in pulls[:6]:
+    for pull in pulls[:urgent]:
         pull.wait()
     pl.semaphore_wait(barrier, count(peers))
 
@@ -136,11 +137,21 @@
     def onward(index, step, there):
         send_kv(whole(index), whole(index), kv_recv.at[index], seq + step * CORES, head, there)
 
-    for d in range(1, kv_heads):
-        other = (g + d) % kv_heads
-        for n, (ref, arrival) in enumerate(((k_buf, kv_recv.at[mine]), (v_buf, v_recv.at[d - 1]))):
-            send_kv(ref.at[:, cols(other)], kv.at[n, span(mine, rows), :], arrival,
-                    seq, other * share + x)
+    def reach(index, step):
+        there = inside(z + step)
+        send_kv(whole(index), whole(index), kv_recv.at[index], seq + step * CORES, head, there)
+
+    def inside(depth):
+        return (depth >= 0) & (depth < deep)
+
+    for turn in range(1, kv_heads):
+        send_kv(stage.at[turn - 1], whole(mine), kv_recv.at[mine], seq,
+                (g + turn) % kv_heads * share + x)
+    along = peers[-2:] if deep > 1 else []
+    if deep > 1:
+        reach(mine, 1)
+        reach(mine, -1)
+        signal(ready.at[0], along)
 
     def chunk_of(lane, core, n):
         return [ref.at[lane, pl.ds(core * q_rows + n * BLOCK, BLOCK), :] for ref in (q_all, do_all)]
@@ -157,12 +168,6 @@
                 send(functools.partial(remote, part, part, x_send.at[slot], x_recv.at[slot], seq,
                                        g * share + (x + d) % share))
 
-    onward(mine, 1, z + 1 < deep)
-    onward(mine, -1, z > 0)
-    for d in range(1, share):
-        slot = far_at + (d - 1) * 2
-        send(functools.partial(remote, lay_in, lay_far.at[d - 1], x_send.at[slot],
-                               x_recv.at[slot], seq, g * share + (x + d) % share))
     send_chunk(0)
     partner = z * CORES + 1 - c
     for n, ref in enumerate((q_all, do_all)):
@@ -170,7 +175,30 @@
         send(functools.partial(remote, part, part, core_send.at[n], core_recv.at[n],
                                partner, head))
 
-    for pull in pulls[6:]:
+    for pull in pulls[urgent:urgent + 2]:
+        pull.wait()
+    queries, blocks = CORES * own, order.shape[0]
+    units = own_tops.shape[0]
+    row_of = lax.broadcasted_iota(jnp.int32, (queries, BLOCK), 0)
+    at_block = jnp.zeros((queries, BLOCK), jnp.int32)
+    for i in range(queries):
+        at_block = jnp.where(row_of == i, order[z * queries + i], at_block)
+    column = lax.broadcasted_iota(jnp.int32, (queries, blocks), 1)
+    picked = jnp.where(column == at_block[:, :blocks], 1.0, 0.0).astype(jnp.bfloat16)
+    for h in range(heads):
+        seen[0, h] = jnp.dot(picked, layout[h].astype(jnp.float32).astype(jnp.bfloat16),
+                             preferred_element_type=jnp.float32)
+    for d in range(1, share):
+        slot = far_at + (d - 1) * 2
+        send(functools.partial(remote, seen.at[0], seen.at[d], x_send.at[slot], x_recv.at[slot],
+                               seq, g * share + (x + d) % share))
+    for d in range(1, min(REACH, deep) - 1):
+        pl.semaphore_wait(ready.at[d - 1], count(along))
+        if d + 2 < min(REACH, deep):
+            signal(ready.at[d], along)
+        reach(mine, d + 1)
+        reach(mine, -d - 1)
+    for pull in pulls[urgent + 2:]:
         pull.wait()
     mine_stats = stats.at[x, pl.ds(c * own, own)]
     for n in range(own):
@@ -192,23 +220,19 @@
     for n in range(1, own):
         send_chunk(n)
 
-    lane_of = lax.broadcasted_iota(jnp.int32, (1, BLOCK), 1)
-
-    def fill_tops(lane):
-        def top_row(i, _):
-            qb = order[z * CORES * own + i]
-
-            def top_unit(u, _):
-                kb = order[unit_row(u, unit, rows, kv_heads, share) // BLOCK]
-                for h in range(heads):
-                    on = layout[lane, h, qb, kb] == 1
-                    at = pl.ds(pl.multiple_of((lane * heads + h) * BLOCK, BLOCK), BLOCK)
-                    tops[i, u, :, at] = jnp.where(on, lane_of + qb * BLOCK, -1)
-                return 0
-
-            return lax.fori_loop(0, tops.shape[1], top_unit, 0)
-
-        lax.fori_loop(0, tops.shape[0], top_row, 0)
+    block_of = lax.broadcasted_iota(jnp.int32, (blocks, BLOCK), 0)
+    chosen = jnp.concatenate([
+        jnp.where(block_of == order[unit_row(u, unit, rows, kv_heads, share) // BLOCK], 1.0, 0.0)
+        for u in range(units)], axis=1).astype(jnp.bfloat16)
+    at_query = at_block * BLOCK + lax.broadcasted_iota(jnp.int32, (queries, BLOCK), 1)
+
+    def fill_tops(ref, slot, source):
+        for h in range(heads):
+            on = jnp.dot(seen[source, h].astype(jnp.bfloat16), chosen,
+                         preferred_element_type=jnp.float32)
+            at = slice((slot * heads + h) * BLOCK, (slot * heads + h + 1) * BLOCK)
+            for u in range(units):
+                ref[u, :, at] = jnp.where(on[:, u * BLOCK:(u + 1) * BLOCK] > 0.5, at_query, -1)
 
     ids = docs[...]
     low = jnp.zeros_like(ids)
@@ -217,6 +241,87 @@
         before = jnp.sum(before, axis=0, keepdims=True).astype(jnp.int32)
         low = jnp.where(ids >= d, before, low)
     lows[...] = low
+    fill_tops(own_tops, 0, 0)
+    acc[...] = jnp.zeros_like(acc)
+    dq_own[...] = jnp.zeros_like(dq_own)
+    low_bits[...] = jnp.zeros_like(low_bits)
+
+    sub = lax.broadcasted_iota(jnp.int32, (unit, SPAN * heads * BLOCK), 0)
+    both = [(j, h) for j in range(SPAN) for h in range(heads)]
+
+    def stacked(ref, t):
+        return jnp.concatenate(
+            [ref[x, pl.ds(pl.multiple_of((t * SPAN + j) * BLOCK, BLOCK), BLOCK),
+                 h * D_HEAD:(h + 1) * D_HEAD] for j, h in both], axis=0)
+
+    def joint(n, batch):
+        return jnp.concatenate([kv[n, span(index, rows), :] for index in batch], axis=0)
+
+    def weigh(t, batch):
+        st = lax.dot_general(joint(0, batch), stacked(q_all, t), NT,
+                             preferred_element_type=jnp.float32)
+        dpt = lax.dot_general(joint(1, batch), stacked(do_all, t), NT,
+                              preferred_element_type=jnp.float32)
+        rowed = [stats[x, t * SPAN + j] for j in range(SPAN)]
+        norm = jnp.concatenate([rowed[j][h:h + 1] for j, h in both], axis=1)
+        delta = jnp.concatenate([rowed[j][heads + h:heads + h + 1] for j, h in both], axis=1)
+        lowed = [lows[pl.ds(order[z * CORES * own + t * SPAN + j], 1), :] for j in range(SPAN)]
+        low = jnp.concatenate([lowed[j] for j, _ in both], axis=1)
+        keeps = []
+        for u in [index * (rows // unit) + n for index in batch for n in range(rows // unit)]:
+            row = unit_row(u, unit, rows, kv_heads, share)
+            pos = order[row // BLOCK] * BLOCK + row % BLOCK
+            top = jnp.concatenate([own_tops[u, pl.ds(t * SPAN + j, 1), :] for j in range(SPAN)], axis=1)
+            keeps.append((sub >= low - pos) & (sub <= top - pos))
+        keep = jnp.concatenate(keeps, axis=0)
+        w = jnp.where(keep, jnp.exp2(st * (SCALE * LOG2E) - norm), 0.0)
+        low_bits[0] = w.astype(jnp.bfloat16)
+        low_bits[1] = (w * (dpt - delta)).astype(jnp.bfloat16)
+
+    def collect(t, batch):
+        ds = low_bits[1]
+        dv = jnp.dot(low_bits[0], stacked(do_all, t), preferred_element_type=jnp.float32)
+        dk = jnp.dot(ds, stacked(q_all, t), preferred_element_type=jnp.float32)
+        dq = lax.dot_general(joint(0, batch), ds, TN, preferred_element_type=jnp.float32)
+        for n, index in enumerate(batch):
+            at, part = span(index, rows), slice(n * rows, (n + 1) * rows)
+            acc[0, at, :] += dk[part]
+            acc[1, at, :] += dv[part]
+        for j in range(SPAN):
+            dq_own[t * SPAN + j] += dq[:, j * heads * BLOCK:(j + 1) * heads * BLOCK]
+
+    turns = queries // SPAN
+
+    def nearest(k):
+        short = jnp.minimum(z, deep - 1 - z)
+        beyond = jnp.where(z < deep - 1 - z, k, deep - 1 - k)
+        return jnp.where(k <= 2 * short, z + (k + 1) // 2 * (1 - 2 * (k % 2)), beyond)
+
+    def of(k, turn):
+        return nearest(k) * kv_heads + (g + turn) % kv_heads
+
+    order_of = [[(0, turn) for turn in range(kv_heads)]]
+    late = 1
+    if kv_heads == 2 and deep > 2:
+        order_of += [[(1, turn), (2, turn)] for turn in range(kv_heads)]
+        late = 3
+    order_of += [[(k, turn) for turn in range(kv_heads)] for k in range(late, deep)]
+    batches = [[of(*entry) for entry in batch] for batch in order_of]
+
+    def attend(k, midway=None):
+        batch, before = batches[k], batches[max(k - 1, 0)]
+
+        def turn(t, _):
+            first = t == 0
+            collect(jnp.where(first, 0 if k == 0 else turns - 1, t - 1),
+                    [jnp.where(first, old, new) for old, new in zip(before, batch)])
+            weigh(t, batch)
+            return 0
+
+        lax.fori_loop(0, turns // 2, turn, 0)
+        if midway is not None:
+            midway()
+        lax.fori_loop(turns // 2, turns, turn, 0)
 
     def relay(part, slot):
         landed(part, x_recv.at[slot])
@@ -230,41 +335,56 @@
 
     for j in range(1, kv_heads):
         index = z * kv_heads + (g + j) % kv_heads
-        for n, sem in enumerate((kv_recv.at[index], v_recv.at[kv_heads - j - 1])):
-            landed(kv.at[n, span(index, rows), :], sem)
-        onward(index, 1, z + 1 < deep)
-        onward(index, -1, z > 0)
-    chunks = 0
-    for d in range(1, deep):
-        for j in range(kv_heads):
-            for depth, step, here_too in ((z - d, 1, z - d >= 0), (z + d, -1, z + d < deep)):
-                index = depth * kv_heads + (g + j) % kv_heads
-                when(here_too, functools.partial(
-                    lambda index: landed(whole(index), kv_recv.at[index]), index))
-                if d < deep - 1:
-                    more = z + 1 < deep if step == 1 else z > 0
-                    onward(index, step, here_too & more)
-        if d == 1:
-            fill_tops(x)
-        if d == min(2, deep - 1):
-            for e in range(1, share):
-                lane = (x - e + share) % share
-                landed(lay_far.at[e - 1], x_recv.at[far_at + (e - 1) * 2])
-                pull = pltpu.make_async_copy(lay_far.at[e - 1], layout.at[lane],
-                                             local.at[len(pulls) + e - 1])
-                pull.start()
-                pull.wait()
-                relay(stats.at[lane, pl.ds(c * own, own)], far_at + (e - 1) * 2 + 1)
-                fill_tops(lane)
-        if chunks < own:
-            relay_chunk(chunks)
-            chunks += 1
-    for n in range(chunks, own):
-        relay_chunk(n)
+        landed(whole(index), kv_recv.at[index])
+        for d in range(1, min(REACH, deep)):
+            reach(index, d)
+            reach(index, -d)
     there = span(1 - c, q_rows)
     for n, ref in enumerate((q_all, do_all)):
         landed(ref.at[x, there, :], core_recv.at[n])
     landed(stats.at[x, pl.ds((1 - c) * own, own)], core_recv.at[2])
+    attend(0)
+
+    def arrive(d, turns_in):
+        for turn in turns_in:
+            for depth, step in ((z - d, 1), (z + d, -1)):
+                index = depth * kv_heads + (g + turn) % kv_heads
+                when(inside(depth), functools.partial(
+                    lambda index: landed(whole(index), kv_recv.at[index]), index))
+                if REACH - 1 <= d < deep - 1:
+                    onward(index, step, inside(depth) & inside(z + step))
+
+    chunks = list(range(own))
+
+    def relay_next():
+        if chunks:
+            relay_chunk(chunks.pop(0))
+
+    def relay_rest():
+        while chunks:
+            relay_chunk(chunks.pop(0))
+
+    done = 1
+    for turns_in in ([0], list(range(1, kv_heads))):
+        for d in range(1, min(REACH, deep)):
+            arrive(d, turns_in)
+        if turns_in == [0]:
+            for e in range(1, share):
+                landed(seen.at[e], x_recv.at[far_at + (e - 1) * 2])
+                fill_tops(tops, e - 1, e)
+                relay(stats.at[(x - e + share) % share, pl.ds(c * own, own)],
+                      far_at + (e - 1) * 2 + 1)
+        relay_next()
+        if late == 3:
+            attend(done)
+            done += 1
+    for d in range(REACH, deep):
+        arrive(d, range(kv_heads))
+    relay_next()
+    for k in range(done, deep):
+        attend(k, relay_rest if k == deep - 1 else None)
+    relay_rest()
+    collect(turns - 1, batches[deep - 1])
     for d in range(1, share):
         lane = (x - d + share) % share
         for n in range(own):
@@ -289,7 +409,7 @@
     vmem = pl.BlockSpec(memory_space=pltpu.VMEM)
     lanes = share - 1
     x_copies = max(1, lanes * own * 2 + lanes * 2)
-    kv_copies = max(1, 2 * (kv_heads - 1) + 2 * kv_heads * (deep - 1))
+    kv_copies = 2 * kv_heads * (deep + REACH)
     dma = pltpu.SemaphoreType.DMA
     every = jax.ShapeDtypeStruct((share, CORES * q_rows, heads * D_HEAD), queries.dtype)
     return pl.pallas_call(
@@ -301,23 +421,26 @@
             jax.ShapeDtypeStruct((share, CORES * own, 2 * heads, BLOCK), jnp.float32),
             jax.ShapeDtypeStruct((blocks, BLOCK), jnp.int32),
             jax.ShapeDtypeStruct(
-                (CORES * own, kv_rows // unit, 1, share * heads * BLOCK), jnp.int32),
-            jax.ShapeDtypeStruct((max(1, lanes),) + block_layout.shape, jnp.int32),
+                (kv_rows // unit, CORES * own, max(1, lanes) * heads * BLOCK), jnp.int32),
+            jax.ShapeDtypeStruct((2, kv_rows, D_HEAD), jnp.float32),
+            jax.ShapeDtypeStruct((CORES * own, D_HEAD, heads * BLOCK), jnp.float32),
         ),
         in_specs=[hbm] * 9,
-        out_specs=(vmem,) * 6 + (hbm,),
+        out_specs=(vmem,) * 8,
         scratch_shapes=[
-            pltpu.VMEM(keys.shape, keys.dtype),
-            pltpu.VMEM(values.shape, values.dtype),
+            pltpu.VMEM((max(1, kv_heads - 1), 2, rows, D_HEAD), keys.dtype),
             pltpu.VMEM(attn_out.shape, attn_out.dtype),
             pltpu.VMEM(log_norm.shape, jnp.float32),
             pltpu.VMEM((blocks, BLOCK), jnp.int32),
             pltpu.SMEM((blocks,), jnp.int32),
-            pltpu.SMEM((share,) + block_layout.shape, jnp.int32),
-            dma((11 + max(1, lanes),)),
+            pltpu.VMEM(block_layout.shape, jnp.int32),
+            pltpu.VMEM((share, heads, CORES * own, blocks), jnp.float32),
+            pltpu.VMEM((kv_rows // unit, CORES * own, heads * BLOCK), jnp.int32),
+            pltpu.VMEM((2, kv_heads * rows, SPAN * heads * BLOCK), jnp.bfloat16),
+            dma((2 * kv_heads + 7,)),
+            pltpu.SemaphoreType.REGULAR((REACH,)),
             dma((kv_copies,)),
             dma((pieces,)),
-            dma((max(1, kv_heads - 1),)),
             dma((x_copies,)),
             dma((x_copies,)),
             dma((3 + x_copies,)),
@@ -332,7 +455,7 @@
 
 
 def grads_kernel(
-    kv_heads, share, rows, order_in, docs_in, q_all, do_all, stats, kv, lows, tops,
+    kv_heads, share, rows, order_in, docs_in, q_all, do_all, stats, kv, lows, tops, acc_in,
     dqt, acc, order, docs, unit_pos, item_q, item_u, low_bits, local,
 ):
     z, c, g, x = place(share)
@@ -341,14 +464,15 @@
     unit = min(rows, BLOCK)
     units = kv.shape[1] // unit
     first = z * queries
+    others = [(x - d + share) % share for d in range(1, share)]
     pulls = [pltpu.make_async_copy(order_in, order, local.at[0]),
              pltpu.make_async_copy(docs_in, docs, local.at[1])]
     for pull in pulls:
         pull.start()
-    acc[...] = jnp.zeros_like(acc)
+    acc[...] = acc_in[...]
 
     def clear(i, _):
-        for s in range(share):
+        for s in range(share - 1):
             dqt[s, pl.ds(i, 1)] = jnp.zeros((1,) + dqt.shape[2:], jnp.float32)
         return 0
 
@@ -372,7 +496,7 @@
         return n
 
     total = lax.fori_loop(0, queries, listing, 0)
-    wide = share * heads * BLOCK
+    wide = (share - 1) * heads * BLOCK
     sub = lax.broadcasted_iota(jnp.int32, (unit, wide), 0)
     low_bits[...] = jnp.zeros_like(low_bits)
     for n in range(2 * PAIR):
@@ -382,7 +506,7 @@
     def stacked(ref, i):
         at = pl.ds(pl.multiple_of(i * BLOCK, BLOCK), BLOCK)
         return jnp.concatenate(
-            [ref[s, at, h * D_HEAD:(h + 1) * D_HEAD] for s in range(share) for h in range(heads)],
+            [ref[s, at, h * D_HEAD:(h + 1) * D_HEAD] for s in others for h in range(heads)],
             axis=0)
 
     def weigh(n, slot):
@@ -391,12 +515,12 @@
         at = pl.ds(pl.multiple_of(u * unit, unit), unit)
         k, v = kv[0, at, :], kv[1, at, :]
         q4, do4 = stacked(q_all, i), stacked(do_all, i)
-        rowed = [stats[s, i] for s in range(share)]
+        rowed = [stats[s, i] for s in others]
         norm = jnp.concatenate([r[h:h + 1] for r in rowed for h in range(heads)], axis=1)
         delta = jnp.concatenate(
             [r[heads + h:heads + h + 1] for r in rowed for h in range(heads)], axis=1)
-        low = jnp.concatenate([lows[pl.ds(order[first + i], 1), :]] * (share * heads), axis=1)
-        top = jnp.where(n < total, tops[i, u], -1)
+        low = jnp.concatenate([lows[pl.ds(order[first + i], 1), :]] * ((share - 1) * heads), axis=1)
+        top = jnp.where(n < total, tops[u, pl.ds(i, 1), :], -1)
         keep = (sub >= low - pos) & (sub <= top - pos)
         st = lax.dot_general(k, q4, NT, preferred_element_type=jnp.float32)
         dpt = lax.dot_general(v, do4, NT, preferred_element_type=jnp.float32)
@@ -422,26 +546,26 @@
         for i, at, dk, dv, dq in done:
             acc[0, at, :] += dk
             acc[1, at, :] += dv
-            for s in range(share):
+            for s in range(share - 1):
                 dqt[s, i] += dq[:, s * heads * BLOCK:(s + 1) * heads * BLOCK]
         return 0
 
     lax.fori_loop(0, (total + PAIR - 1) // PAIR + 1, step, 0)
 
 
-def local_grads(block_order, document_ids, q_all, do_all, stats, kv, lows, tops, rows, kv_heads,
-                share):
+def local_grads(block_order, document_ids, q_all, do_all, stats, kv, lows, tops, acc, rows,
+                kv_heads, share):
     heads = q_all.shape[2] // D_HEAD
-    queries, units = tops.shape[:2]
+    units, queries = tops.shape[:2]
     hbm = pl.BlockSpec(memory_space=pltpu.HBM)
     vmem = pl.BlockSpec(memory_space=pltpu.VMEM)
     return pl.pallas_call(
         functools.partial(grads_kernel, kv_heads, share, rows),
         out_shape=(
-            jax.ShapeDtypeStruct((share, queries, D_HEAD, heads * BLOCK), jnp.float32),
+            jax.ShapeDtypeStruct((share - 1, queries, D_HEAD, heads * BLOCK), jnp.float32),
             jax.ShapeDtypeStruct(kv.shape, jnp.float32),
         ),
-        in_specs=[hbm] * 2 + [vmem] * 6,
+        in_specs=[hbm] * 2 + [vmem] * 7,
         out_specs=(vmem, vmem),
         scratch_shapes=[
             pltpu.SMEM(block_order.shape, jnp.int32),
@@ -449,19 +573,20 @@
             pltpu.SMEM((units,), jnp.int32),
             pltpu.SMEM((queries * units + 2 * PAIR,), jnp.int32),
             pltpu.SMEM((queries * units + 2 * PAIR,), jnp.int32),
-            pltpu.VMEM((PAIR, 2, min(rows, BLOCK), share * heads * BLOCK), jnp.bfloat16),
+            pltpu.VMEM((PAIR, 2, min(rows, BLOCK), (share - 1) * heads * BLOCK),
+                       jnp.bfloat16),
             pltpu.SemaphoreType.DMA((2,)),
         ],
         compiler_params=pltpu.CompilerParams(vmem_limit_bytes=24 << 20),
         name="grads",
     )(pltpu.with_memory_space_constraint(block_order, pltpu.HBM),
       pltpu.with_memory_space_constraint(document_ids, pltpu.HBM),
-      q_all, do_all, stats, kv, lows, tops)
+      q_all, do_all, stats, kv, lows, tops, acc)
 
 
 def scatter_kernel(
-    deep, kv_heads, share, rows, acc, dqt, kv_in, dq_sum, dq_in,
-    kv_out, joined, dq_core, dq_out, ready, kv_send, kv_recv, join_recv, core_send, core_recv,
+    deep, kv_heads, share, rows, acc, dq_own, dqt, kv_in, dq_sum, dq_in,
+    kv_out, joined, own_core, dq_core, dq_out, ready, kv_send, kv_recv, join_recv, core_send, core_recv,
     x_send, x_recv,
 ):
     z, c, g, x = place(share)
@@ -516,8 +641,9 @@
             kv_out[index, n] = (acc[n, at, :] * factor
                                 + joined[index, n].astype(jnp.float32)).astype(jnp.bfloat16)
 
-    def blocks_of(core, n):
-        return dqt.at[:, pl.ds(core * own + n, 1)]
+    def crossing(core, n):
+        at = pl.ds(core * own + n, 1)
+        return ((dqt.at[:, at], dq_core.at[:, pl.ds(n, 1)]), (dq_own.at[at], own_core.at[pl.ds(n, 1)]))
 
     for far in range(deep - 1, REACH - 1, -1):
         for depth, step in ((far, 1), (deep - 1 - far, -1)):
@@ -537,8 +663,9 @@
     for turn in range(1, kv_heads):
         give(0, turn)
     for n in range(own):
-        send(functools.partial(remote, blocks_of(1 - c, n), dq_core.at[:, pl.ds(n, 1)],
-                               core_send.at[n], core_recv.at[n], partner, head))
+        for m, (src, dst) in enumerate(crossing(1 - c, n)):
+            send(functools.partial(remote, src, dst, core_send.at[2 * n + m],
+                                   core_recv.at[2 * n + m], partner, head))
     along = peers[-2:] if deep > 1 else []
     near_end = {1: z == 0, -1: z == deep - 1}
     for d in range(1, min(REACH, deep)):
@@ -553,11 +680,15 @@
                 give(step * (d + 1), 0, there & near_end[step] if d == REACH - 2 else there)
 
     def query_block(n):
-        landed(dq_core.at[:, pl.ds(n, 1)], core_recv.at[n])
+        for m, (_, dst) in enumerate(crossing(1 - c, n)):
+            landed(dst, core_recv.at[2 * n + m])
         at = slice(n * BLOCK, (n + 1) * BLOCK)
         for d in range(share - 1, -1, -1):
-            lane = (x + d) % share
-            total = (dqt[lane, c * own + n] + dq_core[lane, n]) * SCALE
+            lane = (x - d + share) % share
+            if d:
+                total = (dqt[d - 1, c * own + n] + dq_core[d - 1, n]) * SCALE
+            else:
+                total = (dq_own[c * own + n] + own_core[n]) * SCALE
             for h in range(heads):
                 flat = total[:, h * BLOCK:(h + 1) * BLOCK].T
                 if d:
@@ -611,7 +742,7 @@
             ref[:, j * D_HEAD:(j + 1) * D_HEAD] = total
 
 
-def scatter(dqt, acc, rows, deep, kv_heads, share):
+def scatter(dq_own, dqt, acc, rows, deep, kv_heads, share):
     pieces = deep * kv_heads
     queries, heads = dqt.shape[1], dqt.shape[3] // BLOCK
     own = queries // CORES
@@ -626,26 +757,27 @@
             jax.ShapeDtypeStruct((q_rows, heads * D_HEAD), jnp.float32),
             jax.ShapeDtypeStruct((lanes, q_rows, heads * D_HEAD), jnp.bfloat16),
         ),
-        in_specs=[vmem] * 2,
+        in_specs=[vmem] * 3,
         out_specs=(vmem,) * 3,
         scratch_shapes=[
             pltpu.VMEM((pieces, 2, rows, D_HEAD), jnp.bfloat16),
             pltpu.VMEM((pieces, 2, rows, D_HEAD), jnp.bfloat16),
+            pltpu.VMEM((own,) + dqt.shape[2:], jnp.float32),
             pltpu.VMEM((dqt.shape[0], own) + dqt.shape[2:], jnp.float32),
             pltpu.VMEM((lanes, q_rows, heads * D_HEAD), jnp.bfloat16),
             pltpu.SemaphoreType.REGULAR((max(1, deep - 1),)),
             dma((6 * pieces,)),
             dma((pieces,)),
             dma((pieces,)),
-            dma((own,)),
-            dma((own,)),
+            dma((2 * own,)),
+            dma((2 * own,)),
             dma((lanes * own,)),
             dma((lanes * own,)),
         ],
         compiler_params=pltpu.CompilerParams(collective_id=1, has_side_effects=True,
             vmem_limit_bytes=20 << 20),
         name="scatter",
-    )(acc, dqt)
+    )(acc, dq_own, dqt)
     grad = jax.ShapeDtypeStruct((rows, kv_heads * D_HEAD), jnp.float32)
     return pl.pallas_call(
         functools.partial(finish_kernel, deep, kv_heads, share),
@@ -664,12 +796,12 @@
     kv_heads = lax.axis_size("head") // share
     deep = lax.axis_size("seq") // CORES
     rows = keys.shape[0]
-    kv, q_all, do_all, stats, lows, tops, _ = gather(
+    kv, q_all, do_all, stats, lows, tops, acc, dq_own = gather(
         queries, out_grad, attn_out, log_norm, keys, values, block_layout, document_ids,
         block_order, deep, kv_heads, share)
-    dqt, acc = local_grads(block_order, document_ids, q_all, do_all, stats, kv, lows, tops, rows,
-                           kv_heads, share)
-    return tuple(scatter(dqt, acc, rows, deep, kv_heads, share))
+    dqt, acc = local_grads(block_order, document_ids, q_all, do_all, stats, kv, lows, tops, acc,
+                           rows, kv_heads, share)
+    return tuple(scatter(dq_own, dqt, acc, rows, deep, kv_heads, share))
 
 
 def solution(mesh):

time: 43.3 us -> 40.3 us (0.931); the launches traced: 43.5 us -> 39.8 us
  Pallas kernels: 42.8 us -> 39.1 us
    pallas_call x1, Pallas kernels: 5.65 us -> 2.99 us  [local_grads(): pl.pallas_call(functools.partial(grads_kernel, kv_heads, share, rows), ou...]
    pallas_call x1, Pallas kernels: 15.6 us -> 14.7 us  [scatter(): pl.pallas_call(functools.partial(scatter_kernel, deep, kv_heads, share, r...]
where the time goes in v1:
time: 40.3 us; the launch traced here: 39.8 us
  Pallas kernels  39.1 us (97%)
  between operations  0.66 us (2%)
    pallas_call x1, Pallas kernels, gather(): pl.pallas_call(functools.partial(gather_kernel, deep, kv_heads, share), o...  20.5 us
    pallas_call x1, Pallas kernels, scatter(): pl.pallas_call(functools.partial(scatter_kernel, deep, kv_heads, share, r...  14.7 us
    pallas_call x1, Pallas kernels, local_grads(): pl.pallas_call(functools.partial(grads_kernel, kv_heads, share, rows), ou...  2.99 us
    pallas_call x1, Pallas kernels, scatter(): pl.pallas_call(functools.partial(finish_kernel, deep, kv_heads, share), o...  0.93 us

profile of v1, /device:TPU:0, one launch (start us, length us, event | category | flops | bytes accessed | tf_op | source)
XLA Modules:
  0.0 39.8 jit_solution(3295570715522507824)
XLA Ops:
  0.6 20.5 %gather.1 = (bf16[2,1024,128]{2,1,0:T(8,128)(2,1)S(1)}, bf16[2,1024,256]{2,1,0:T(8,128)(2,1)S(1)}, bf16[2,1024,256]{2,1,0:T(8,128)(2,1)S(1)}, f32[2,8,4,128]{3,2...) custom-call(bf16[512,256]{1,0:T(8,128)(2,1)} %q_in.1, ...), custom_call_target="tpu_custom_call" | custom-call | tf_op jit(solution)/shard_map/gather/pallas_call | solution.py:415
  21.1 3.0 %grads.1 = (f32[1,8,128,256]{3,2,1,0:T(8,128)S(1)}, f32[2,1024,128]{2,1,0:T(8,128)S(1)}) custom-call(s32[32]{0:T(128)} %order_in.3, s32[4096]{0:T(1024)} %docs_in.1, bf16[2,1024,256]{2,1,0:T(8,128)(2,1)S(1)} %get-tuple-element.16.q_all, bf16[2,1024,256]{2,1,0:T(8,128)(2,1)S(1)} %get-tuple-element.17.do_all, f32[2,8,4,128]{3,2,1,0:T(4,128)S(1)} %get-tuple-element.18.stats, ...), custom_call_target="tpu_custom_call" | custom-call | tf_op jit(solution)/shard_map/grads/pallas_call | solution.py:562
  24.2 14.7 %scatter.1 = (bf16[8,2,128,128]{3,2,1,0:T(8,128)(2,1)S(1)}, f32[512,256]{1,0:T(8,128)S(1)}, bf16[1,512,256]{2,1,0:T(8,128)(2,1)S(1)}) custom-call(f32[2,1024,128]{2,1,0:T(8,128)S(1)} %get-tuple-element.23.acc, f32[8,128,256]{2,1,0:T(8,128)S(1)} %get-tuple-element.24.dq_own, f32[1,8,128,256]{3,2,1,0:T(8,128)S(1)} %get-tuple-element.25.dqt), custom_call_target="tpu_custom_call" | custom-call | tf_op jit(solution)/shard_map/scatter/pallas_call | solution.py:753
  38.9 0.9 %finish.1 = (f32[512,256]{1,0:T(8,128)}, f32[128,256]{1,0:T(8,128)}, f32[128,256]{1,0:T(8,128)}) custom-call(bf16[8,2,128,128]{3,2,1,0:T(8,128)(2,1)S(1)} %get-tuple-element.26.kv_in, f32[512,256]{1,0:T(8,128)S(1)} %get-tuple-element.27.dq_sum, bf16[1,512,256]{2,1,0:T(8,128)(2,1)S(1)} %get-tuple-element.28.dq_in), custom_call_target="tpu_custom_call" | custom-call | tf_op jit(solution)/shard_map/finish/pallas_call | solution.py:782
